TPU v7x, 32 devices: a whole 2x2x4 slice. The times are simulated.
32 devices in a mesh: grp: 2 (over y), blk: 4 (over z), uly: 4 (over x, core).
Axes of the slice: x: 2, y: 2, z: 4, core: 2. Of those that a mesh axis runs over, the one named last changes fastest.
Arguments:
- qkv: bfloat16 [2, 8, 16, 3, 32, 128], P('grp', 'blk', 'uly'), parts along dimension 0, may hold values from -6 to 6
- out_weight: bfloat16 [4096, 256], replicated, may hold values from -0.25 to 0.25
- lift_weight: bfloat16 [64, 512], P(None, 'uly'), may hold values from -0.75 to 0.75
- conv_weight: bfloat16 [4, 3, 3, 512, 512], P(None, None, None, 'uly'), may hold values from -0.15625 to 0.15625
Outputs:
- pixels: bfloat16 [2, 16, 32, 512], P('grp', 'blk', None, 'uly'), parts along dimension 0
There are 2 independent parts, one for each index of `grp`. A program takes and returns all parts, laid end to end along the dimension named above; an argument that names none is the same for every part. Nothing has to cross between parts.
All inputs are finite; a program needn't handle non-finite values.
Results may differ from a plain program's by a relative error of at most 0.02.
Values may be sent and summed in bfloat16 or wider, within the bound.
A program may use at most 64 MiB of HBM per device.

v0:
```python
import functools

import jax
import jax.numpy as jnp
from jax import lax
from jax.sharding import PartitionSpec as P

PATCH = 2
LAYERS = 4


def with_halo(cells, sides, width):
    for axis, dim in sides:
        count = lax.axis_size(axis)
        ends = count - 1
        head = lax.slice_in_dim(cells, 0, width, axis=dim)
        tail = lax.slice_in_dim(cells, cells.shape[dim] - width, cells.shape[dim], axis=dim)
        cells = jnp.concatenate(
            [
                lax.ppermute(tail, axis, [(i, (i + 1) % count) for i in range(ends)]),
                cells,
                lax.ppermute(head, axis, [((i + 1) % count, i) for i in range(ends)]),
            ],
            axis=dim,
        )
    return cells


def online_update(carry, pieces, start, queries, scale):
    highest, totals, summed = carry
    keys = pieces[0].reshape(-1, pieces[0].shape[-2], pieces[0].shape[-1])
    values = pieces[1].reshape(-1, pieces[1].shape[-2], pieces[1].shape[-1])
    scores = jnp.einsum("qhd,khd->hqk", queries, keys, preferred_element_type=jnp.float32) * scale
    new_high = jnp.maximum(highest, jnp.max(scores, axis=2))
    weights = jnp.exp(scores - new_high[:, :, None])
    totals = jnp.sum(weights, axis=2)
    update = jnp.einsum(
        "hqk,khd->qhd", weights.astype(jnp.bfloat16), values, preferred_element_type=jnp.float32
    )
    summed = update
    return (new_high, totals, summed)


def attention_start(flat_queries):
    count, heads, size = flat_queries.shape
    return (
        jnp.full((heads, count), -1e30, jnp.float32),
        jnp.zeros((heads, count), jnp.float32),
        jnp.zeros((count, heads, size), jnp.float32),
    )


def attention_finish(carry, shape):
    highest, totals, summed = carry
    return (summed / jnp.transpose(totals)[:, :, None]).astype(jnp.bfloat16).reshape(shape)


def unfold_patches(piece, latent_ch):
    frames, rows, cols = (piece.shape[0], piece.shape[1], piece.shape[2])
    spread = piece.reshape(frames, rows, cols, PATCH, PATCH, latent_ch)
    spread = jnp.transpose(spread, (0, 1, 3, 2, 4, 5))
    return spread.reshape(frames, rows * PATCH, cols * PATCH, latent_ch)


def conv_layer(current, kernels):
    rims = with_halo(current, (("blk", 1),), 1)
    frames, height, width, outputs = current.shape
    empty = jnp.zeros((frames, height, width, outputs), jnp.float32)
    summed = empty
    padded = jnp.pad(
        lax.all_gather(rims, "uly", axis=3, tiled=True), ((0, 0), (0, 0), (1, 1), (0, 0))
    )
    for above in range(3):
        for beside in range(3):
            window = padded[:, above : above + height, beside : beside + width, :]
            summed = summed + jnp.einsum(
                "fyxc,dc->fyxd", window, kernels[above, beside], preferred_element_type=jnp.float32
            )
    return jax.nn.silu(summed).astype(jnp.bfloat16)


def body(qkv, out_weight, lift_weight, conv_weight):
    scale = 1.0 / qkv.shape[-1] ** 0.5
    grouped = lax.all_to_all(qkv, "blk", split_axis=4, concat_axis=1, tiled=True)
    queries = grouped[:, :, :, 0]
    flat_queries = queries.reshape(-1, queries.shape[3], queries.shape[4])
    folding = functools.partial(online_update, queries=flat_queries, scale=scale)
    carry = folding(
        attention_start(flat_queries),
        (
            lax.all_gather(grouped[:, :, :, 1], "uly", axis=2, tiled=True),
            lax.all_gather(grouped[:, :, :, 2], "uly", axis=2, tiled=True),
        ),
        jnp.int32(0),
    )
    attended = attention_finish(carry, queries.shape)
    restored = lax.all_to_all(attended, "blk", split_axis=1, concat_axis=3, tiled=True)
    frames, rows, cols = (restored.shape[0], restored.shape[1], restored.shape[2])
    features = restored.reshape(frames, rows, cols, restored.shape[3] * restored.shape[4])
    patches = jnp.einsum(
        "frcw,wp->frcp", features, out_weight, preferred_element_type=jnp.float32
    ).astype(jnp.bfloat16)
    latent_ch = lift_weight.shape[0]
    latent = unfold_patches(lax.all_gather(patches, "uly", axis=2, tiled=True), latent_ch)
    current = jnp.einsum(
        "fyxe,ed->fyxd", latent, lift_weight, preferred_element_type=jnp.float32
    ).astype(jnp.bfloat16)
    for layer in range(LAYERS):
        current = conv_layer(current, conv_weight[layer])
    return current


def solution(mesh):
    in_specs = (
        P("grp", "blk", "uly", None, None, None),
        P(),
        P(None, "uly"),
        P(None, None, None, "uly", None),
    )
    out_specs = P("grp", "blk", None, "uly")
    return jax.shard_map(body, mesh=mesh, in_specs=in_specs, out_specs=out_specs, check_vma=False)
```

profile of v0, /device:TPU:0, one launch (start us, length us, event | category | flops | bytes accessed | tf_op | source)
XLA Modules:
  0.0 105.2 jit_solution(9364590570968090370)
XLA Ops:
  0.0 1.2 %copy.17 = bf16[1,2,4,3,32,128]{5,2,3,1,0,4:T(4,128)(2,1)S(1)} copy(bf16[1,2,4,3,32,128]{5,4,3,2,1,0:T(8,128)(2,1)} %param.4) | data formatting | bytes 393216 | tf_op args[0]
  1.2 13.6 %all_to_all.33 = bf16[1,2,4,3,32,128]{5,2,3,1,0,4:T(4,128)(2,1)S(1)} all-to-all(bf16[1,2,4,3,32,128]{5,2,3,1,0,4:T(4,128)(2,1)S(1)} %copy.17), channel_id=1, replica_groups=mesh['grp'=2,'blk'=4,'uly'=4] {'blk'}, dimensions={4} | all-to-all | bytes 393216 | tf_op jit(solution)/shard_map/all_to_all | solution.py:84
  14.9 5.8 %all-gather = bf16[1,8,16,1,8,128]{5,4,3,1,0,2:T(8,128)(2,1)S(1)} all-gather(bf16[1,8,4,1,8,128]{5,4,3,1,0,2:T(8,128)(2,1)S(1)} %get-tuple-element.9), channel_id=2, replica_groups=mesh['grp'=2,'blk'=4,'uly'=4] {'uly'}, dimensions={2}, use_global_device_ids=true | all-gather | bytes 327680 | tf_op jit(solution)/shard_map/all_gather | solution.py:91
  20.9 0.3 fusion.114
  21.2 5.9 %all-gather.1 = bf16[1,8,16,1,8,128]{5,4,3,1,0,2:T(8,128)(2,1)S(1)} all-gather(bf16[1,8,4,1,8,128]{5,4,3,1,0,2:T(8,128)(2,1)S(1)} %get-tuple-element.10), channel_id=3, replica_groups=mesh['grp'=2,'blk'=4,'uly'=4] {'uly'}, dimensions={2}, use_global_device_ids=true | all-gather | bytes 327680 | tf_op jit(solution)/shard_map/all_gather | solution.py:92
  27.3 0.2 fusion.60
  27.5 0.2 fusion.3
  27.8 8.3 %all_to_all.34 = bf16[1,8,4,8,128]{4,2,3,0,1:T(4,128)(2,1)S(1)} all-to-all(bf16[1,8,4,8,128]{4,2,3,0,1:T(4,128)(2,1)S(1)} %copy.22), channel_id=1, replica_groups=mesh['grp'=2,'blk'=4,'uly'=4] {'blk'}, dimensions={1} | all-to-all | bytes 131072 | tf_op jit(solution)/shard_map/all_to_all | solution.py:97
  36.1 0.4 fusion.5
  36.5 5.2 %all-gather.2 = bf16[2,16,256]{2,0,1:T(2,128)(2,1)S(1)} all-gather(bf16[2,4,256]{2,0,1:T(2,128)(2,1)S(1)} %copy.24), channel_id=4, replica_groups=mesh['grp'=2,'blk'=4,'uly'=4] {'uly'}, dimensions={1}, use_global_device_ids=true | all-gather | bytes 20480 | tf_op jit(solution)/shard_map/all_gather | solution.py:104
  42.0 2.8 %collective-permute-start = (bf16[1,1,32,128]{3,2,1,0:T(8,128)(2,1)S(1)}, bf16[1,1,32,128]{3,2,1,0:T(8,128)(2,1)S(1)}, u32[]{:S(2)}, u32[]{:S(2)}) collective-permute-start(bf16[1,1,32,128]{3,2,1,0:T(8,128)(2,1)S(1)} %get-tuple-element.18), channel_id=1, source_target_pairs={{0,4},{4,8},{8,12},{1,5},{5,9},{9,13},{2,6},{6,10},{10,14},{3,7},{... | collective-permute-start | bytes 24584 | tf_op jit(solution)/shard_map/ppermute | solution.py:20
  44.8 1.3 %collective-permute-start.1 = (bf16[1,1,32,128]{3,2,1,0:T(8,128)(2,1)S(1)}, bf16[1,1,32,128]{3,2,1,0:T(8,128)(2,1)S(1)}, u32[]{:S(2)}, u32[]{:S(2)}) collective-permute-start(bf16[1,1,32,128]{3,2,1,0:T(8,128)(2,1)S(1)} %get-tuple-element.19), channel_id=1, source_target_pairs={{4,0},{8,4},{12,8},{5,1},{9,5},{13,9},{6,2},{10,6},{14,10},{7,3},{... | collective-permute-start | bytes 24584 | tf_op jit(solution)/shard_map/ppermute | solution.py:22
  46.1 2.6 %slice_bitcast_fusion = (bf16[3,3,128,512]{3,2,1,0:T(8,128)(2,1)S(1)}, bf16[3,3,128,512]{3,2,1,0:T(8,128)(2,1)S(1)}, bf16[3,3,128,512]{3,2,1,0:T(8,128)(2,1)S(1)}, bf16[3,3,128,512]{3,2,1,0:T(8,128)(2,1)S(1)}) fusion(bf16[4,3,3,128,512]{4,3,2,1,0:T(8,128)(2,1)} %param.7), kind=kLoop, calls=%fused_computation.2 | loop fusion | bytes 9437184 | tf_op jit(solution)/shard_map/squeeze | solution.py:109
  48.8 1.6 %collective-permute-done.1 = bf16[1,1,32,128]{3,2,1,0:T(8,128)(2,1)S(1)} collective-permute-done((bf16[1,1,32,128]{3,2,1,0:T(8,128)(2,1)S(1)}, bf16[1,1,32,128]{3,2,1,0:T(8,128)(2,1)S(1)}, u32[]{:S(2)}, u32[]{:S(2)}) %collective-permute-start.1) | collective-permute-done | bytes 8224 | tf_op jit(solution)/shard_map/ppermute | solution.py:22
  50.4 5.6 %all_gather.24 = bf16[1,6,32,512]{3,2,1,0:T(8,128)(2,1)S(1)} all-gather(bf16[1,6,32,128]{3,2,1,0:T(8,128)(2,1)S(1)} %pad_maximum_fusion), channel_id=1, replica_groups=mesh['grp'=2,'blk'=4,'uly'=4] {'uly'}, dimensions={3}, use_global_device_ids=true | all-gather | bytes 245760 | tf_op jit(solution)/shard_map/all_gather | solution.py:71
  56.2 0.2 convolution_add_fusion.31
  56.8 0.2 convolution_add_fusion.28
  57.0 0.2 convolution_add_fusion.27
  57.1 0.2 convolution_add_fusion.26
  57.3 0.2 convolution_add_fusion.25
  57.5 0.2 fusion.80
  57.8 3.0 %collective-permute-start.2 = (bf16[1,1,32,128]{3,2,1,0:T(8,128)(2,1)S(1)}, bf16[1,1,32,128]{3,2,1,0:T(8,128)(2,1)S(1)}, u32[]{:S(2)}, u32[]{:S(2)}) collective-permute-start(bf16[1,1,32,128]{3,2,1,0:T(8,128)(2,1)S(1)} %get-tuple-element.16), channel_id=1, source_target_pairs={{0,4},{4,8},{8,12},{1,5},{5,9},{9,13},{2,6},{6,10},{10,14},{3,7},{... | collective-permute-start | bytes 24584 | tf_op jit(solution)/shard_map/ppermute | solution.py:20
  60.7 1.3 %collective-permute-start.3 = (bf16[1,1,32,128]{3,2,1,0:T(8,128)(2,1)S(1)}, bf16[1,1,32,128]{3,2,1,0:T(8,128)(2,1)S(1)}, u32[]{:S(2)}, u32[]{:S(2)}) collective-permute-start(bf16[1,1,32,128]{3,2,1,0:T(8,128)(2,1)S(1)} %get-tuple-element.17), channel_id=1, source_target_pairs={{4,0},{8,4},{12,8},{5,1},{9,5},{13,9},{6,2},{10,6},{14,10},{7,3},{... | collective-permute-start | bytes 24584 | tf_op jit(solution)/shard_map/ppermute | solution.py:22
  62.1 4.2 %collective-permute-done.3 = bf16[1,1,32,128]{3,2,1,0:T(8,128)(2,1)S(1)} collective-permute-done((bf16[1,1,32,128]{3,2,1,0:T(8,128)(2,1)S(1)}, bf16[1,1,32,128]{3,2,1,0:T(8,128)(2,1)S(1)}, u32[]{:S(2)}, u32[]{:S(2)}) %collective-permute-start.3) | collective-permute-done | bytes 8224 | tf_op jit(solution)/shard_map/ppermute | solution.py:22
  66.3 5.6 %all_gather.25 = bf16[1,6,32,512]{3,2,1,0:T(8,128)(2,1)S(1)} all-gather(bf16[1,6,32,128]{3,2,1,0:T(8,128)(2,1)S(1)} %pad_maximum_fusion.1), channel_id=1, replica_groups=mesh['grp'=2,'blk'=4,'uly'=4] {'uly'}, dimensions={3}, use_global_device_ids=true | all-gather | bytes 245760 | tf_op jit(solution)/shard_map/all_gather | solution.py:71
  72.1 0.2 convolution_add_fusion.23
  72.7 0.2 convolution_add_fusion.20
  72.9 0.2 convolution_add_fusion.19
  73.3 0.2 convolution_add_fusion.17
  73.5 0.2 fusion.75
  73.7 2.3 %collective-permute-start.4 = (bf16[1,1,32,128]{3,2,1,0:T(8,128)(2,1)S(1)}, bf16[1,1,32,128]{3,2,1,0:T(8,128)(2,1)S(1)}, u32[]{:S(2)}, u32[]{:S(2)}) collective-permute-start(bf16[1,1,32,128]{3,2,1,0:T(8,128)(2,1)S(1)} %get-tuple-element.14), channel_id=1, source_target_pairs={{0,4},{4,8},{8,12},{1,5},{5,9},{9,13},{2,6},{6,10},{10,14},{3,7},{... | collective-permute-start | bytes 24584 | tf_op jit(solution)/shard_map/ppermute | solution.py:20
  76.0 1.3 %collective-permute-start.5 = (bf16[1,1,32,128]{3,2,1,0:T(8,128)(2,1)S(1)}, bf16[1,1,32,128]{3,2,1,0:T(8,128)(2,1)S(1)}, u32[]{:S(2)}, u32[]{:S(2)}) collective-permute-start(bf16[1,1,32,128]{3,2,1,0:T(8,128)(2,1)S(1)} %get-tuple-element.15), channel_id=1, source_target_pairs={{4,0},{8,4},{12,8},{5,1},{9,5},{13,9},{6,2},{10,6},{14,10},{7,3},{... | collective-permute-start | bytes 24584 | tf_op jit(solution)/shard_map/ppermute | solution.py:22
  77.4 4.2 %collective-permute-done.5 = bf16[1,1,32,128]{3,2,1,0:T(8,128)(2,1)S(1)} collective-permute-done((bf16[1,1,32,128]{3,2,1,0:T(8,128)(2,1)S(1)}, bf16[1,1,32,128]{3,2,1,0:T(8,128)(2,1)S(1)}, u32[]{:S(2)}, u32[]{:S(2)}) %collective-permute-start.5) | collective-permute-done | bytes 8224 | tf_op jit(solution)/shard_map/ppermute | solution.py:22
  81.6 5.6 %all_gather.26 = bf16[1,6,32,512]{3,2,1,0:T(8,128)(2,1)S(1)} all-gather(bf16[1,6,32,128]{3,2,1,0:T(8,128)(2,1)S(1)} %pad_maximum_fusion.2), channel_id=1, replica_groups=mesh['grp'=2,'blk'=4,'uly'=4] {'uly'}, dimensions={3}, use_global_device_ids=true | all-gather | bytes 245760 | tf_op jit(solution)/shard_map/all_gather | solution.py:71
  87.6 0.2 convolution_add_fusion.14
  87.8 0.2 convolution_add_fusion.13
  88.2 0.2 convolution_add_fusion.11
  88.5 0.2 convolution_add_fusion.9
  88.7 0.2 fusion.70
  89.0 2.6 %collective-permute-start.6 = (bf16[1,1,32,128]{3,2,1,0:T(8,128)(2,1)S(1)}, bf16[1,1,32,128]{3,2,1,0:T(8,128)(2,1)S(1)}, u32[]{:S(2)}, u32[]{:S(2)}) collective-permute-start(bf16[1,1,32,128]{3,2,1,0:T(8,128)(2,1)S(1)} %get-tuple-element.12), channel_id=1, source_target_pairs={{0,4},{4,8},{8,12},{1,5},{5,9},{9,13},{2,6},{6,10},{10,14},{3,7},{... | collective-permute-start | bytes 24584 | tf_op jit(solution)/shard_map/ppermute | solution.py:20
  91.6 1.3 %collective-permute-start.7 = (bf16[1,1,32,128]{3,2,1,0:T(8,128)(2,1)S(1)}, bf16[1,1,32,128]{3,2,1,0:T(8,128)(2,1)S(1)}, u32[]{:S(2)}, u32[]{:S(2)}) collective-permute-start(bf16[1,1,32,128]{3,2,1,0:T(8,128)(2,1)S(1)} %get-tuple-element.13), channel_id=1, source_target_pairs={{4,0},{8,4},{12,8},{5,1},{9,5},{13,9},{6,2},{10,6},{14,10},{7,3},{... | collective-permute-start | bytes 24584 | tf_op jit(solution)/shard_map/ppermute | solution.py:22
  93.0 4.2 %collective-permute-done.7 = bf16[1,1,32,128]{3,2,1,0:T(8,128)(2,1)S(1)} collective-permute-done((bf16[1,1,32,128]{3,2,1,0:T(8,128)(2,1)S(1)}, bf16[1,1,32,128]{3,2,1,0:T(8,128)(2,1)S(1)}, u32[]{:S(2)}, u32[]{:S(2)}) %collective-permute-start.7) | collective-permute-done | bytes 8224 | tf_op jit(solution)/shard_map/ppermute | solution.py:22
  97.2 5.6 %all_gather.27 = bf16[1,6,32,512]{3,2,1,0:T(8,128)(2,1)S(1)} all-gather(bf16[1,6,32,128]{3,2,1,0:T(8,128)(2,1)S(1)} %pad_maximum_fusion.3), channel_id=1, replica_groups=mesh['grp'=2,'blk'=4,'uly'=4] {'uly'}, dimensions={3}, use_global_device_ids=true | all-gather | bytes 245760 | tf_op jit(solution)/shard_map/all_gather | solution.py:71
  103.2 0.2 convolution_add_fusion.6
  103.4 0.2 convolution_add_fusion.5
  103.8 0.2 convolution_add_fusion.3
  104.1 0.2 convolution_add_fusion.1
  104.3 0.8 fusion.65
  (44 shorter events, 3.8 us)
Async XLA Ops:
  0.0 36.1 %copy-start = (bf16[4096,256]{1,0:T(8,128)(2,1)S(1)}, bf16[4096,256]{1,0:T(8,128)(2,1)}, u32[]{:S(2)}) copy-start(bf16[4096,256]{1,0:T(8,128)(2,1)} %param.5) | copy-start | bytes 6291460
  36.1 5.8 %copy-start.1 = (bf16[64,128]{1,0:T(8,128)(2,1)S(1)}, bf16[64,128]{1,0:T(8,128)(2,1)}, u32[]{:S(2)}) copy-start(bf16[64,128]{1,0:T(8,128)(2,1)} %param.6) | copy-start | bytes 49156
  42.0 6.8 %collective-permute-start = (bf16[1,1,32,128]{3,2,1,0:T(8,128)(2,1)S(1)}, bf16[1,1,32,128]{3,2,1,0:T(8,128)(2,1)S(1)}, u32[]{:S(2)}, u32[]{:S(2)}) collective-permute-start(bf16[1,1,32,128]{3,2,1,0:T(8,128)(2,1)S(1)} %get-tuple-element.18), channel_id=1, source_target_pairs={{0,4},{4,8},{8,12},{1,5},{5,9},{9,13},{2,6},{6,10},{10,14},{3,7},{... | collective-permute-start | bytes 24584 | tf_op jit(solution)/shard_map/ppermute | solution.py:20
  44.8 5.5 %collective-permute-start.1 = (bf16[1,1,32,128]{3,2,1,0:T(8,128)(2,1)S(1)}, bf16[1,1,32,128]{3,2,1,0:T(8,128)(2,1)S(1)}, u32[]{:S(2)}, u32[]{:S(2)}) collective-permute-start(bf16[1,1,32,128]{3,2,1,0:T(8,128)(2,1)S(1)} %get-tuple-element.19), channel_id=1, source_target_pairs={{4,0},{8,4},{12,8},{5,1},{9,5},{13,9},{6,2},{10,6},{14,10},{7,3},{... | collective-permute-start | bytes 24584 | tf_op jit(solution)/shard_map/ppermute | solution.py:22
  57.8 4.3 %collective-permute-start.2 = (bf16[1,1,32,128]{3,2,1,0:T(8,128)(2,1)S(1)}, bf16[1,1,32,128]{3,2,1,0:T(8,128)(2,1)S(1)}, u32[]{:S(2)}, u32[]{:S(2)}) collective-permute-start(bf16[1,1,32,128]{3,2,1,0:T(8,128)(2,1)S(1)} %get-tuple-element.16), channel_id=1, source_target_pairs={{0,4},{4,8},{8,12},{1,5},{5,9},{9,13},{2,6},{6,10},{10,14},{3,7},{... | collective-permute-start | bytes 24584 | tf_op jit(solution)/shard_map/ppermute | solution.py:20
  60.7 5.5 %collective-permute-start.3 = (bf16[1,1,32,128]{3,2,1,0:T(8,128)(2,1)S(1)}, bf16[1,1,32,128]{3,2,1,0:T(8,128)(2,1)S(1)}, u32[]{:S(2)}, u32[]{:S(2)}) collective-permute-start(bf16[1,1,32,128]{3,2,1,0:T(8,128)(2,1)S(1)} %get-tuple-element.17), channel_id=1, source_target_pairs={{4,0},{8,4},{12,8},{5,1},{9,5},{13,9},{6,2},{10,6},{14,10},{7,3},{... | collective-permute-start | bytes 24584 | tf_op jit(solution)/shard_map/ppermute | solution.py:22
  73.7 3.7 %collective-permute-start.4 = (bf16[1,1,32,128]{3,2,1,0:T(8,128)(2,1)S(1)}, bf16[1,1,32,128]{3,2,1,0:T(8,128)(2,1)S(1)}, u32[]{:S(2)}, u32[]{:S(2)}) collective-permute-start(bf16[1,1,32,128]{3,2,1,0:T(8,128)(2,1)S(1)} %get-tuple-element.14), channel_id=1, source_target_pairs={{0,4},{4,8},{8,12},{1,5},{5,9},{9,13},{2,6},{6,10},{10,14},{3,7},{... | collective-permute-start | bytes 24584 | tf_op jit(solution)/shard_map/ppermute | solution.py:20
  76.0 5.5 %collective-permute-start.5 = (bf16[1,1,32,128]{3,2,1,0:T(8,128)(2,1)S(1)}, bf16[1,1,32,128]{3,2,1,0:T(8,128)(2,1)S(1)}, u32[]{:S(2)}, u32[]{:S(2)}) collective-permute-start(bf16[1,1,32,128]{3,2,1,0:T(8,128)(2,1)S(1)} %get-tuple-element.15), channel_id=1, source_target_pairs={{4,0},{8,4},{12,8},{5,1},{9,5},{13,9},{6,2},{10,6},{14,10},{7,3},{... | collective-permute-start | bytes 24584 | tf_op jit(solution)/shard_map/ppermute | solution.py:22
  89.0 4.0 %collective-permute-start.6 = (bf16[1,1,32,128]{3,2,1,0:T(8,128)(2,1)S(1)}, bf16[1,1,32,128]{3,2,1,0:T(8,128)(2,1)S(1)}, u32[]{:S(2)}, u32[]{:S(2)}) collective-permute-start(bf16[1,1,32,128]{3,2,1,0:T(8,128)(2,1)S(1)} %get-tuple-element.12), channel_id=1, source_target_pairs={{0,4},{4,8},{8,12},{1,5},{5,9},{9,13},{2,6},{6,10},{10,14},{3,7},{... | collective-permute-start | bytes 24584 | tf_op jit(solution)/shard_map/ppermute | solution.py:20
  91.6 5.5 %collective-permute-start.7 = (bf16[1,1,32,128]{3,2,1,0:T(8,128)(2,1)S(1)}, bf16[1,1,32,128]{3,2,1,0:T(8,128)(2,1)S(1)}, u32[]{:S(2)}, u32[]{:S(2)}) collective-permute-start(bf16[1,1,32,128]{3,2,1,0:T(8,128)(2,1)S(1)} %get-tuple-element.13), channel_id=1, source_target_pairs={{4,0},{8,4},{12,8},{5,1},{9,5},{13,9},{6,2},{10,6},{14,10},{7,3},{... | collective-permute-start | bytes 24584 | tf_op jit(solution)/shard_map/ppermute | solution.py:22
where the time goes:
time: 106 us; the launch traced here: 105 us
  blocking collectives  61.2 us (58%)
  starting transfers between devices  15.9 us (15%)
  waiting for transfers between devices  14.3 us (13%)
  matrix products  8.44 us (8%)
  local copies, waits for them, and re-layouts  4.51 us (4%)
    all_gather x4, blocking collectives, conv_layer(): lax.all_gather(rims, 'uly', axis=3, tiled=True)  22.5 us
    ppermute x4, waiting for transfers between devices, with_halo(): lax.ppermute(head, axis, [((i + 1) % count, i) for i in range(ends)])  14.2 us
    all_to_all x1, blocking collectives, body(): lax.all_to_all(qkv, 'blk', split_axis=4, concat_axis=1, tiled=True)  13.6 us
    ppermute x4, starting transfers between devices, with_halo(): lax.ppermute(tail, axis, [(i, (i + 1) % count) for i in range(ends)])  10.8 us
    all_to_all x1, blocking collectives, body(): lax.all_to_all(attended, 'blk', split_axis=1, concat_axis=3, tiled=True)  8.26 us
    dot_general x36, matrix products, conv_layer(): jnp.einsum('fyxc,dc->fyxd', window, kernels[above, beside], preferred_ele...  7.35 us
    all_gather x1, blocking collectives, body(): lax.all_gather(grouped[:, :, :, 2], 'uly', axis=2, tiled=True)  5.85 us
    all_gather x1, blocking collectives, body(): lax.all_gather(grouped[:, :, :, 1], 'uly', axis=2, tiled=True)  5.78 us
  transfers between devices with their start and end apart: 8, of which 4 were waited for; matrix products, arithmetic and copies ran while one was open for 3% of the time, Pallas kernels for 0%

commit v1 on v0

--- a/solution.py
+++ b/solution.py
@@ -2,7 +2,10 @@
 
 import jax
 import jax.numpy as jnp
+import numpy as np
 from jax import lax
+from jax.experimental import pallas as pl
+from jax.experimental.pallas import tpu as pltpu
 from jax.sharding import PartitionSpec as P
 
 PATCH = 2
@@ -79,7 +82,7 @@
     return jax.nn.silu(summed).astype(jnp.bfloat16)
 
 
-def body(qkv, out_weight, lift_weight, conv_weight):
+def body_by_steps(qkv, out_weight, lift_weight, conv_weight):
     scale = 1.0 / qkv.shape[-1] ** 0.5
     grouped = lax.all_to_all(qkv, "blk", split_axis=4, concat_axis=1, tiled=True)
     queries = grouped[:, :, :, 0]
@@ -110,6 +113,263 @@
     return current
 
 
+MESH = pl.DeviceIdType.MESH
+NT = (((1,), (1,)), ((), ()))
+
+
+def remote(src, dst, send, recv, target):
+    return pltpu.make_async_remote_copy(
+        src_ref=src, dst_ref=dst, send_sem=send, recv_sem=recv, device_id=target, device_id_type=MESH
+    )
+
+
+def fused_kernel(
+    cfg, qkv, out_w, lift_w, conv_w, sel, keep, out,
+    qkv_all, out_v, lift_all, conv_v, sel_v, keep_v, att_mine, att_all, patch_mine, patch_all, x0, acts,
+    local_sem, q_send, q_recv, l_send, l_recv, a_send, a_recv, p_send, p_recv, c_send, c_recv,
+):
+    nb, nu, hp, size, own, width = cfg
+    nd = nb * nu
+    blk, uly = lax.axis_index("blk"), lax.axis_index("uly")
+    me = blk * nu + uly
+    count = qkv_all.shape[3]
+    f32, bf16 = jnp.float32, jnp.bfloat16
+
+    order = [(db, du) for db in sorted(range(nb), key=lambda d: -min(d, nb - d)) for du in range(nu) if db + du > 0]
+    others = []
+    for db, du in order:
+        tb, tu = lax.rem(blk + db, nb), lax.rem(uly + du, nu)
+        others.append((tb * nu + tu, {"blk": tb, "uly": tu}))
+    peers = [lax.rem(uly + du, nu) for du in range(1, nu)]
+
+    patch_all[...] = jnp.zeros_like(patch_all)
+    barrier = pltpu.get_barrier_semaphore()
+    for _, target in others:
+        pl.semaphore_signal(barrier, inc=1, device_id=target, device_id_type=MESH)
+
+    mine = pltpu.make_async_copy(qkv.at[me], qkv_all.at[me], local_sem.at[0])
+    mine.start()
+    lift_own = pltpu.make_async_copy(lift_w, lift_all.at[uly], local_sem.at[1])
+    lift_own.start()
+    loads = [
+        pltpu.make_async_copy(a, b, local_sem.at[2 + i])
+        for i, (a, b) in enumerate(((out_w, out_v), (sel, sel_v), (keep, keep_v)))
+    ]
+    conv_loads = [
+        pltpu.make_async_copy(conv_w.at[layer], conv_v.at[layer], local_sem.at[5 + layer]) for layer in range(LAYERS)
+    ]
+    pl.semaphore_wait(barrier, nd - 1)
+
+    sent = []
+    for where, target in others:
+        copy = remote(qkv.at[where], qkv_all.at[me], q_send.at[where], q_recv.at[me], target)
+        copy.start()
+        sent.append(copy)
+    for peer in peers:
+        copy = remote(lift_w, lift_all.at[uly], l_send.at[peer], l_recv.at[uly], {"uly": peer})
+        copy.start()
+        sent.append(copy)
+    for copy in loads + conv_loads:
+        copy.start()
+
+    mine.wait()
+    for where, target in others:
+        remote(qkv.at[where], qkv_all.at[where], q_send.at[where], q_recv.at[where], target).wait_recv()
+
+    scale = 1.0 / size**0.5
+    for head in range(hp):
+        q, k, v = (
+            qkv_all[:, part, head].astype(f32).reshape(nd * count, size).astype(bf16) for part in range(3)
+        )
+        scores = lax.dot_general(q, k, NT, preferred_element_type=f32) * scale
+        weights = jnp.exp(scores - jnp.max(scores, axis=1, keepdims=True))
+        totals = jnp.sum(weights, axis=1, keepdims=True)
+        mixed = jnp.dot(weights.astype(bf16), v, preferred_element_type=f32) / totals
+        att_mine[:, :, head * size : (head + 1) * size] = mixed.reshape(nd, count, size).astype(bf16)
+
+    for where, target in others:
+        copy = remote(att_mine.at[where], att_all.at[me], a_send.at[where], a_recv.at[me], target)
+        copy.start()
+        sent.append(copy)
+
+    for copy in loads:
+        copy.wait()
+    total = jnp.dot(att_mine[me], out_v[me], preferred_element_type=f32)
+    for where, target in reversed(others):
+        remote(att_mine.at[where], att_all.at[where], a_send.at[where], a_recv.at[where], target).wait_recv()
+        total = total + jnp.dot(att_all[where], out_v[where], preferred_element_type=f32)
+    patch = total.astype(bf16)
+    patch_mine[...] = patch
+    patch_all[1, uly] = patch
+
+    def patch_copy(db, tu, slot, lane):
+        return remote(
+            patch_mine, patch_all.at[slot, lane], p_send.at[db + 1, tu], p_recv.at[slot, lane],
+            {"blk": blk + db, "uly": tu},
+        )
+
+    reach = ((-1, blk > 0), (1, blk < nb - 1))
+    for db, inside in reach:
+
+        @pl.when(inside)
+        def _():
+            for tu in range(nu):
+                patch_copy(db, tu, 1 - db, uly).start()
+
+    for peer in peers:
+        copy = remote(patch_mine, patch_all.at[1, uly], p_send.at[1, peer], p_recv.at[1, uly], {"uly": peer})
+        copy.start()
+        sent.append(copy)
+    lift_own.wait()
+    for peer in peers:
+        remote(lift_w, lift_all.at[peer], l_send.at[peer], l_recv.at[peer], {"uly": peer}).wait_recv()
+    lift = jnp.concatenate([lift_all[u] for u in range(nu)], axis=1)
+    lift = jnp.concatenate([lift] * (PATCH * PATCH), axis=0)
+    for peer in peers:
+        remote(
+            patch_mine, patch_all.at[1, peer], p_send.at[1, peer], p_recv.at[1, peer], {"uly": peer}
+        ).wait_recv()
+    for db, inside in reach:
+
+        @pl.when(inside)
+        def _():
+            for tu in range(nu):
+                copy = patch_copy(db, tu, 1 + db, tu)
+                copy.wait_recv()
+                copy.wait_send()
+
+    patches = patch_all[...].astype(f32).reshape(-1, patch_all.shape[-1]).astype(bf16)
+    spread = jnp.dot(sel_v[...], patches, preferred_element_type=f32).astype(bf16) * keep_v[...]
+    x0[...] = jnp.dot(spread, lift, preferred_element_type=f32).astype(bf16)
+
+    for layer in range(LAYERS):
+        edge = LAYERS - 1 - layer
+        span = (own + 2 * edge) * width
+        conv_loads[layer].wait()
+        acc = None
+        for above in range(3):
+            rows = slice(above * width, above * width + span)
+            if layer == 0:
+                window = x0[rows, :]
+            else:
+                window = jnp.concatenate([acts[layer - 1][u, rows, :] for u in range(nu)], axis=1)
+            part = lax.dot_general(window, conv_v[layer, above], NT, preferred_element_type=f32)
+            acc = part if acc is None else acc + part
+        outs = acc.shape[1] // 3
+        place = lax.broadcasted_iota(jnp.int32, (span, outs), 0)
+        column = place & (width - 1)
+        left = jnp.where(column == 0, 0.0, pltpu.roll(acc[:, :outs], 1, 0))
+        right = jnp.where(column == width - 1, 0.0, pltpu.roll(acc[:, 2 * outs :], span - 1, 0))
+        z = acc[:, outs : 2 * outs] + left + right
+        y = z / (1.0 + jnp.exp(-z))
+        if edge == 0:
+            out[...] = y.astype(bf16)
+            break
+        place = place + (blk * own - edge) * width
+        y = jnp.where((place >= 0) & (place < nb * own * width), y, 0.0).astype(bf16)
+        act = acts[layer]
+        act[uly] = y
+        for peer in peers:
+            copy = remote(
+                act.at[uly], act.at[uly], c_send.at[layer, peer], c_recv.at[layer, uly], {"uly": peer}
+            )
+            copy.start()
+            sent.append(copy)
+        for peer in peers:
+            remote(
+                act.at[peer], act.at[peer], c_send.at[layer, peer], c_recv.at[layer, peer], {"uly": peer}
+            ).wait_recv()
+
+    for copy in sent:
+        copy.wait_send()
+
+
+def spread_tables(nu, rows, cols, latent_ch):
+    own = PATCH * rows
+    width = PATCH * cols * nu
+    y, w = np.meshgrid(np.arange(own - LAYERS, 2 * own + LAYERS), np.arange(width), indexing="ij")
+    y, w = y.reshape(-1), w.reshape(-1)
+    slot, row = np.divmod(y // PATCH, rows)
+    lane, col = np.divmod(w // PATCH, cols)
+    token = ((slot * nu + lane) * rows + row) * cols + col
+    sel = token[:, None] == np.arange(3 * nu * rows * cols)[None]
+    piece = (y % PATCH) * PATCH + w % PATCH
+    keep = piece[:, None] == (np.arange(PATCH * PATCH * latent_ch) // latent_ch)[None]
+    return jnp.asarray(sel, jnp.bfloat16), jnp.asarray(keep, jnp.bfloat16)
+
+
+def body_fused(nb, nu, qkv, out_weight, lift_weight, conv_weight):
+    _, rows, cols, _, heads, size = qkv.shape
+    nd, count = nb * nu, rows * cols
+    hp = heads // nd
+    own, width = PATCH * rows, PATCH * cols * nu
+    latent_ch, outs = lift_weight.shape
+    channels = conv_weight.shape[4]
+    feats = out_weight.shape[1]
+    blocks = jnp.transpose(qkv.reshape(count, 3, nd, hp, size), (2, 1, 3, 0, 4))
+    sel, keep = spread_tables(nu, rows, cols, latent_ch)
+    bf16 = jnp.bfloat16
+    dma = pltpu.SemaphoreType.DMA
+    anywhere = pl.BlockSpec(memory_space=pl.ANY)
+    pixels = pl.pallas_call(
+        functools.partial(fused_kernel, (nb, nu, hp, size, own, width)),
+        out_shape=jax.ShapeDtypeStruct((own * width, outs), bf16),
+        in_specs=[anywhere] * 6,
+        out_specs=pl.BlockSpec(memory_space=pltpu.VMEM),
+        scratch_shapes=[
+            pltpu.VMEM((nd, 3, hp, count, size), bf16),
+            pltpu.VMEM((nd, hp * size, feats), bf16),
+            pltpu.VMEM((nu, latent_ch, outs), bf16),
+            pltpu.VMEM((LAYERS, 3, 3 * outs, channels), bf16),
+            pltpu.VMEM(sel.shape, bf16),
+            pltpu.VMEM(keep.shape, bf16),
+            pltpu.VMEM((nd, count, hp * size), bf16),
+            pltpu.VMEM((nd, count, hp * size), bf16),
+            pltpu.VMEM((count, feats), bf16),
+            pltpu.VMEM((3, nu, count, feats), bf16),
+            pltpu.VMEM(((own + 2 * LAYERS) * width, channels), bf16),
+            [
+                pltpu.VMEM((nu, (own + 2 * (LAYERS - 1 - layer)) * width, outs), bf16)
+                for layer in range(LAYERS - 1)
+            ],
+            dma((5 + LAYERS,)),
+            dma((nd,)), dma((nd,)), dma((nu,)), dma((nu,)), dma((nd,)), dma((nd,)),
+            dma((3, nu)), dma((3, nu)), dma((LAYERS - 1, nu)), dma((LAYERS - 1, nu)),
+        ],
+        compiler_params=pltpu.CompilerParams(
+            collective_id=0, has_side_effects=True, vmem_limit_bytes=60 * 1024 * 1024
+        ),
+    )(
+        blocks,
+        out_weight.reshape(nd, hp * size, feats),
+        lift_weight,
+        conv_weight.reshape(LAYERS, 3, 3 * outs, channels),
+        sel,
+        keep,
+    )
+    return pixels.reshape(1, own, width, outs)
+
+
+def body(nb, nu, qkv, out_weight, lift_weight, conv_weight):
+    frames, rows, cols, _, heads, size = qkv.shape
+    width = PATCH * cols * nu
+    fits = (
+        frames == 1
+        and nb > 1
+        and nu > 1
+        and heads % (nb * nu) == 0
+        and (rows * cols) % 8 == 0
+        and size % 128 == 0
+        and lift_weight.shape[1] % 128 == 0
+        and PATCH * rows >= LAYERS
+        and width % 16 == 0
+        and width & (width - 1) == 0
+    )
+    if fits:
+        return body_fused(nb, nu, qkv, out_weight, lift_weight, conv_weight)
+    return body_by_steps(qkv, out_weight, lift_weight, conv_weight)
+
+
 def solution(mesh):
     in_specs = (
         P("grp", "blk", "uly", None, None, None),
@@ -118,4 +378,5 @@
         P(None, None, None, "uly", None),
     )
     out_specs = P("grp", "blk", None, "uly")
-    return jax.shard_map(body, mesh=mesh, in_specs=in_specs, out_specs=out_specs, check_vma=False)
+    step = functools.partial(body, mesh.shape["blk"], mesh.shape["uly"])
+    return jax.shard_map(step, mesh=mesh, in_specs=in_specs, out_specs=out_specs, check_vma=False)

time: 106 us -> 42 us (0.40)
  blocking collectives: 61.2 us -> 0 us
  Pallas kernels: 0 us -> 38.6 us
  starting transfers between devices: 15.9 us -> 0 us
  waiting for transfers between devices: 14.3 us -> 0 us
  matrix products: 8.44 us -> 0 us
  local copies, waits for them, and re-layouts: 4.51 us -> 3.05 us
    all_gather x7 -> x0, blocking collectives: 39.4 us -> none  [the longest x4 22.5 us: conv_layer(): lax.all_gather(rims, 'uly', axis=3, tiled=True)]
    pallas_call x0 -> x1, Pallas kernels: none -> 38.6 us  [body_fused(): pl.pallas_call(functools.partial(fused_kernel, (nb, nu, hp, size, own, wi...]
    all_to_all x2 -> x0, blocking collectives: 21.9 us -> none  [the longest x1 13.6 us: body(): lax.all_to_all(qkv, 'blk', split_axis=4, concat_axis=1, tiled=True)]
    ppermute x8 -> x0, starting transfers between devices: 15.9 us -> none  [the longest x4 10.8 us: with_halo(): lax.ppermute(tail, axis, [(i, (i + 1) % count) for i in range(ends)])]
    ppermute x8 -> x0, waiting for transfers between devices: 14.3 us -> none  [the longest x4 14.2 us: with_halo(): lax.ppermute(head, axis, [((i + 1) % count, i) for i in range(ends)])]
    dot_general x40 -> x0, matrix products: 8.44 us -> none  [the longest x36 7.35 us: conv_layer(): jnp.einsum('fyxc,dc->fyxd', window, kernels[above, beside], preferred_ele...]
    squeeze x1 -> x0, local copies, waits for them, and re-layouts: 2.65 us -> none  [body(): current = conv_layer(current, conv_weight[layer])]
    reshape x3 -> x1, local copies, waits for them, and re-layouts: 0.15 us -> 1.67 us  [body_fused(): blocks = jnp.transpose(qkv.reshape(count, 3, nd, hp, size), (2, 1, 3, 0, 4))]
  transfers between devices with their start and end apart: 8 -> 0, of which waited for: 4 -> 0; matrix products, arithmetic and copies ran while one was open for 3% -> 0% of each run, Pallas kernels for 0% -> 0%
where the time goes in v1:
time: 42 us; the launch traced here: 41.6 us
  Pallas kernels  38.6 us (92%)
  local copies, waits for them, and re-layouts  3.05 us (7%)
    pallas_call x1, Pallas kernels, body_fused(): pl.pallas_call(functools.partial(fused_kernel, (nb, nu, hp, size, own, wi...  38.6 us
    reshape x1, local copies, waits for them, and re-layouts, body_fused(): blocks = jnp.transpose(qkv.reshape(count, 3, nd, hp, size), (2, 1, 3, 0, 4))  1.67 us
    unnamed x1, local copies, waits for them, and re-layouts  1.38 us

profile of v1, /device:TPU:0, one launch (start us, length us, event | category | flops | bytes accessed | tf_op | source)
XLA Modules:
  0.0 41.6 jit_solution(14465743751728541377)
XLA Ops:
  0.0 1.7 %copy.9 = bf16[8,3,16,2,128]{4,0,3,1,2:T(8,128)(2,1)} copy(bf16[8,3,16,2,128]{4,3,2,1,0:T(2,128)(2,1)} %bitcast.10) | data formatting | bytes 393216 | tf_op jit(solution)/shard_map/reshape | solution.py:309
  1.7 38.6 %shard_map.64 = bf16[128,128]{1,0:T(8,128)(2,1)} custom-call(bf16[16,3,2,8,128]{4,3,2,1,0:T(8,128)(2,1)} %bitcast.9, bf16[16,256,256]{2,1,0:T(8,128)(2,1)} %bitcast.8, bf16[64,128]{1,0:T(8,128)(2,1)} %lift_w.1, bf16[4,3,384,512]{3,2,1,0:T(8,128)(2,1)} %bitcast.7, bf16[384,96]{1,0:T(8,128)(2,1)} %constant.4.clone.sel, bf16[384,256]{1,0:T(8,128)(2,1)} %constant.5.clone.keep), custom_call_target="tpu_custom_call" | custom-call | tf_op jit(solution)/shard_map/pallas_call | solution.py:314
  40.2 1.4 %copy.11 = bf16[1,4,32,128]{3,2,1,0:T(8,128)(2,1)} copy(bf16[1,4,32,128]{3,2,1,0:T(8,128)(2,1)} %bitcast.11) | data formatting | bytes 65536

commit v2 on v1

--- a/solution.py
+++ b/solution.py
@@ -125,10 +125,10 @@
 
 def fused_kernel(
     cfg, qkv, out_w, lift_w, conv_w, sel, keep, out,
-    qkv_all, out_v, lift_all, conv_v, sel_v, keep_v, att_mine, att_all, patch_mine, patch_all, x0, acts,
+    qkv_raw, qkv_wide, qkv_mine, qkv_all, out_v, lift_all, conv_v, sel_v, keep_v, att_mine, att_all, patch_mine, patch_all, x0, acts,
     local_sem, q_send, q_recv, l_send, l_recv, a_send, a_recv, p_send, p_recv, c_send, c_recv,
 ):
-    nb, nu, hp, size, own, width = cfg
+    nb, nu, hp, size, own, width, step = cfg
     nd = nb * nu
     blk, uly = lax.axis_index("blk"), lax.axis_index("uly")
     me = blk * nu + uly
@@ -142,13 +142,13 @@
         others.append((tb * nu + tu, {"blk": tb, "uly": tu}))
     peers = [lax.rem(uly + du, nu) for du in range(1, nu)]
 
+    raw = pltpu.make_async_copy(qkv, qkv_raw, local_sem.at[0])
+    raw.start()
     patch_all[...] = jnp.zeros_like(patch_all)
     barrier = pltpu.get_barrier_semaphore()
     for _, target in others:
         pl.semaphore_signal(barrier, inc=1, device_id=target, device_id_type=MESH)
 
-    mine = pltpu.make_async_copy(qkv.at[me], qkv_all.at[me], local_sem.at[0])
-    mine.start()
     lift_own = pltpu.make_async_copy(lift_w, lift_all.at[uly], local_sem.at[1])
     lift_own.start()
     loads = [
@@ -158,23 +158,29 @@
     conv_loads = [
         pltpu.make_async_copy(conv_w.at[layer], conv_v.at[layer], local_sem.at[5 + layer]) for layer in range(LAYERS)
     ]
+    for copy in loads + conv_loads:
+        copy.start()
+    raw.wait()
+    qkv_wide[...] = qkv_raw[...].astype(f32)
+    heads = nd * hp
+    for part in range(3):
+        for head in range(heads):
+            tokens = qkv_wide[pl.ds(part * heads + head, count, stride=3 * heads), :]
+            qkv_mine[head // hp, part, head % hp] = tokens.astype(bf16)
     pl.semaphore_wait(barrier, nd - 1)
 
     sent = []
     for where, target in others:
-        copy = remote(qkv.at[where], qkv_all.at[me], q_send.at[where], q_recv.at[me], target)
+        copy = remote(qkv_mine.at[where], qkv_all.at[me], q_send.at[where], q_recv.at[me], target)
         copy.start()
         sent.append(copy)
     for peer in peers:
         copy = remote(lift_w, lift_all.at[uly], l_send.at[peer], l_recv.at[uly], {"uly": peer})
         copy.start()
         sent.append(copy)
-    for copy in loads + conv_loads:
-        copy.start()
-
-    mine.wait()
+    qkv_all[me] = qkv_mine[me]
     for where, target in others:
-        remote(qkv.at[where], qkv_all.at[where], q_send.at[where], q_recv.at[where], target).wait_recv()
+        remote(qkv_mine.at[where], qkv_all.at[where], q_send.at[where], q_recv.at[where], target).wait_recv()
 
     scale = 1.0 / size**0.5
     for head in range(hp):
@@ -244,41 +250,52 @@
 
     for layer in range(LAYERS):
         edge = LAYERS - 1 - layer
-        span = (own + 2 * edge) * width
+        span = step * width
         conv_loads[layer].wait()
-        acc = None
-        for above in range(3):
-            rows = slice(above * width, above * width + span)
-            if layer == 0:
-                window = x0[rows, :]
-            else:
-                window = jnp.concatenate([acts[layer - 1][u, rows, :] for u in range(nu)], axis=1)
-            part = lax.dot_general(window, conv_v[layer, above], NT, preferred_element_type=f32)
-            acc = part if acc is None else acc + part
-        outs = acc.shape[1] // 3
-        place = lax.broadcasted_iota(jnp.int32, (span, outs), 0)
-        column = place & (width - 1)
-        left = jnp.where(column == 0, 0.0, pltpu.roll(acc[:, :outs], 1, 0))
-        right = jnp.where(column == width - 1, 0.0, pltpu.roll(acc[:, 2 * outs :], span - 1, 0))
-        z = acc[:, outs : 2 * outs] + left + right
-        y = z / (1.0 + jnp.exp(-z))
-        if edge == 0:
-            out[...] = y.astype(bf16)
-            break
-        place = place + (blk * own - edge) * width
-        y = jnp.where((place >= 0) & (place < nb * own * width), y, 0.0).astype(bf16)
-        act = acts[layer]
-        act[uly] = y
-        for peer in peers:
-            copy = remote(
-                act.at[uly], act.at[uly], c_send.at[layer, peer], c_recv.at[layer, uly], {"uly": peer}
-            )
-            copy.start()
-            sent.append(copy)
-        for peer in peers:
-            remote(
-                act.at[peer], act.at[peer], c_send.at[layer, peer], c_recv.at[layer, peer], {"uly": peer}
-            ).wait_recv()
+        chunks = (own + 2 * edge) // step
+        ready = 0
+        for chunk in range(chunks):
+            base = chunk * span
+            if layer > 0:
+                while ready * step < (chunk + 1) * step + 2:
+                    rows = slice(ready * span, (ready + 1) * span)
+                    for peer in peers:
+                        part = acts[layer - 1].at[peer, rows]
+                        remote(
+                            part, part, c_send.at[layer - 1, ready, peer], c_recv.at[layer - 1, ready, peer],
+                            {"uly": peer},
+                        ).wait_recv()
+                    ready += 1
+            acc = None
+            for above in range(3):
+                rows = slice(base + above * width, base + above * width + span)
+                if layer == 0:
+                    window = x0[rows, :]
+                else:
+                    window = jnp.concatenate([acts[layer - 1][u, rows, :] for u in range(nu)], axis=1)
+                part = lax.dot_general(window, conv_v[layer, above], NT, preferred_element_type=f32)
+                acc = part if acc is None else acc + part
+            outs = acc.shape[1] // 3
+            place = lax.broadcasted_iota(jnp.int32, (span, outs), 0)
+            column = place & (width - 1)
+            left = jnp.where(column == 0, 0.0, pltpu.roll(acc[:, :outs], 1, 0))
+            right = jnp.where(column == width - 1, 0.0, pltpu.roll(acc[:, 2 * outs :], span - 1, 0))
+            z = acc[:, outs : 2 * outs] + left + right
+            y = z / (1.0 + jnp.exp(-z))
+            if edge == 0:
+                out[base : base + span, :] = y.astype(bf16)
+                continue
+            place = place + (base + (blk * own - edge) * width)
+            y = jnp.where((place >= 0) & (place < nb * own * width), y, 0.0).astype(bf16)
+            rows = slice(base, base + span)
+            acts[layer][uly, rows, :] = y
+            for peer in peers:
+                part = acts[layer].at[uly, rows]
+                copy = remote(
+                    part, part, c_send.at[layer, chunk, peer], c_recv.at[layer, chunk, uly], {"uly": peer}
+                )
+                copy.start()
+                sent.append(copy)
 
     for copy in sent:
         copy.wait_send()
@@ -303,20 +320,25 @@
     nd, count = nb * nu, rows * cols
     hp = heads // nd
     own, width = PATCH * rows, PATCH * cols * nu
+    step = 2
+    most = (own + 2 * LAYERS) // step
     latent_ch, outs = lift_weight.shape
     channels = conv_weight.shape[4]
     feats = out_weight.shape[1]
-    blocks = jnp.transpose(qkv.reshape(count, 3, nd, hp, size), (2, 1, 3, 0, 4))
+    tokens = qkv.reshape(count * 3 * heads, size)
     sel, keep = spread_tables(nu, rows, cols, latent_ch)
     bf16 = jnp.bfloat16
     dma = pltpu.SemaphoreType.DMA
     anywhere = pl.BlockSpec(memory_space=pl.ANY)
     pixels = pl.pallas_call(
-        functools.partial(fused_kernel, (nb, nu, hp, size, own, width)),
+        functools.partial(fused_kernel, (nb, nu, hp, size, own, width, step)),
         out_shape=jax.ShapeDtypeStruct((own * width, outs), bf16),
         in_specs=[anywhere] * 6,
         out_specs=pl.BlockSpec(memory_space=pltpu.VMEM),
         scratch_shapes=[
+            pltpu.VMEM(tokens.shape, bf16),
+            pltpu.VMEM(tokens.shape, jnp.float32),
+            pltpu.VMEM((nd, 3, hp, count, size), bf16),
             pltpu.VMEM((nd, 3, hp, count, size), bf16),
             pltpu.VMEM((nd, hp * size, feats), bf16),
             pltpu.VMEM((nu, latent_ch, outs), bf16),
@@ -334,13 +356,13 @@
             ],
             dma((5 + LAYERS,)),
             dma((nd,)), dma((nd,)), dma((nu,)), dma((nu,)), dma((nd,)), dma((nd,)),
-            dma((3, nu)), dma((3, nu)), dma((LAYERS - 1, nu)), dma((LAYERS - 1, nu)),
+            dma((3, nu)), dma((3, nu)), dma((LAYERS - 1, most, nu)), dma((LAYERS - 1, most, nu)),
         ],
         compiler_params=pltpu.CompilerParams(
             collective_id=0, has_side_effects=True, vmem_limit_bytes=60 * 1024 * 1024
         ),
     )(
-        blocks,
+        tokens,
         out_weight.reshape(nd, hp * size, feats),
         lift_weight,
         conv_weight.reshape(LAYERS, 3, 3 * outs, channels),
@@ -362,6 +384,7 @@
         and size % 128 == 0
         and lift_weight.shape[1] % 128 == 0
         and PATCH * rows >= LAYERS
+        and PATCH * rows % 2 == 0
         and width % 16 == 0
         and width & (width - 1) == 0
     )

time: 42 us -> 39.6 us (0.943)
  local copies, waits for them, and re-layouts: 3.05 us -> 1.38 us
  Pallas kernels: 38.6 us -> 38.1 us
    reshape x1 -> x0, local copies, waits for them, and re-layouts: 1.67 us -> none  [body_fused(): blocks = jnp.transpose(qkv.reshape(count, 3, nd, hp, size), (2, 1, 3, 0, 4))]
    pallas_call x1, Pallas kernels: 38.6 us -> 38.1 us  [body_fused(): pl.pallas_call(functools.partial(fused_kernel, (nb, nu, hp, size, own, wi...]
where the time goes in v2:
time: 39.6 us; the launch traced here: 39.5 us
  Pallas kernels  38.1 us (96%)
  local copies, waits for them, and re-layouts  1.38 us (3%)
    pallas_call x1, Pallas kernels, body_fused(): pl.pallas_call(functools.partial(fused_kernel, (nb, nu, hp, size, own, wi...  38.1 us
    unnamed x1, local copies, waits for them, and re-layouts  1.38 us

profile of v2, /device:TPU:0, one launch (start us, length us, event | category | flops | bytes accessed | tf_op | source)
XLA Modules:
  0.0 39.5 jit_solution(4538370613969897549)
XLA Ops:
  0.0 38.1 %shard_map.64 = bf16[128,128]{1,0:T(8,128)(2,1)} custom-call(bf16[768,128]{1,0:T(8,128)(2,1)} %bitcast.6, bf16[16,256,256]{2,1,0:T(8,128)(2,1)} %bitcast.5, bf16[64,128]{1,0:T(8,128)(2,1)} %lift_w.1, bf16[4,3,384,512]{3,2,1,0:T(8,128)(2,1)} %bitcast.4, bf16[384,96]{1,0:T(8,128)(2,1)} %constant.4.clone.sel, bf16[384,256]{1,0:T(8,128)(2,1)} %constant.5.clone.keep), custom_call_target="tpu_custom_call" | custom-call | tf_op jit(solution)/shard_map/pallas_call | solution.py:333
  38.1 1.4 %copy.8 = bf16[1,4,32,128]{3,2,1,0:T(8,128)(2,1)} copy(bf16[1,4,32,128]{3,2,1,0:T(8,128)(2,1)} %bitcast.7) | data formatting | bytes 65536

commit v3 on v2

--- a/solution.py
+++ b/solution.py
@@ -126,7 +126,7 @@
 def fused_kernel(
     cfg, qkv, out_w, lift_w, conv_w, sel, keep, out,
     qkv_raw, qkv_wide, qkv_mine, qkv_all, out_v, lift_all, conv_v, sel_v, keep_v, att_mine, att_all, patch_mine, patch_all, x0, acts,
-    local_sem, q_send, q_recv, l_send, l_recv, a_send, a_recv, p_send, p_recv, c_send, c_recv,
+    local_sem, q_send, q_recv, l_send, l_recv, a_send, a_recv, p_send, p_recv, c_send, c_recv, f_send,
 ):
     nb, nu, hp, size, own, width, step = cfg
     nd = nb * nu
@@ -248,18 +248,38 @@
     spread = jnp.dot(sel_v[...], patches, preferred_element_type=f32).astype(bf16) * keep_v[...]
     x0[...] = jnp.dot(spread, lift, preferred_element_type=f32).astype(bf16)
 
+    span = step * width
+    mate = uly + 1 - 2 * lax.rem(uly, 2)
+    alike = [lax.rem(uly + du, nu) for du in range(2, nu, 2)]
+    near = alike + [mate]
+    far = [mate] + [lax.rem(mate + du, nu) for du in range(2, nu, 2)]
+
+    def pass_on(layer, chunk):
+        for peer in alike:
+            part = acts[layer].at[peer, pl.ds(chunk * span, span)]
+            remote(
+                part, part, c_send.at[layer, chunk, peer], c_recv.at[layer, chunk, peer], {"uly": peer}
+            ).wait_recv()
+            copy = remote(
+                part, part, f_send.at[chunk, peer], c_recv.at[layer, chunk, peer], {"uly": mate}
+            )
+            copy.start()
+            sent.append(copy)
+
     for layer in range(LAYERS):
         edge = LAYERS - 1 - layer
-        span = step * width
         conv_loads[layer].wait()
         chunks = (own + 2 * edge) // step
-        ready = 0
+        ready = passed = 0
         for chunk in range(chunks):
             base = chunk * span
             if layer > 0:
                 while ready * step < (chunk + 1) * step + 2:
+                    while layer == 1 and passed < min(ready + 3, chunks + 1):
+                        pass_on(layer - 1, passed)
+                        passed += 1
                     rows = slice(ready * span, (ready + 1) * span)
-                    for peer in peers:
+                    for peer in far if layer == 1 else peers:
                         part = acts[layer - 1].at[peer, rows]
                         remote(
                             part, part, c_send.at[layer - 1, ready, peer], c_recv.at[layer - 1, ready, peer],
@@ -289,7 +309,7 @@
             y = jnp.where((place >= 0) & (place < nb * own * width), y, 0.0).astype(bf16)
             rows = slice(base, base + span)
             acts[layer][uly, rows, :] = y
-            for peer in peers:
+            for peer in near if layer == 0 else peers:
                 part = acts[layer].at[uly, rows]
                 copy = remote(
                     part, part, c_send.at[layer, chunk, peer], c_recv.at[layer, chunk, uly], {"uly": peer}
@@ -332,7 +352,7 @@
     anywhere = pl.BlockSpec(memory_space=pl.ANY)
     pixels = pl.pallas_call(
         functools.partial(fused_kernel, (nb, nu, hp, size, own, width, step)),
-        out_shape=jax.ShapeDtypeStruct((own * width, outs), bf16),
+        out_shape=pltpu.VMEM((own * width, outs), bf16),
         in_specs=[anywhere] * 6,
         out_specs=pl.BlockSpec(memory_space=pltpu.VMEM),
         scratch_shapes=[
@@ -356,7 +376,7 @@
             ],
             dma((5 + LAYERS,)),
             dma((nd,)), dma((nd,)), dma((nu,)), dma((nu,)), dma((nd,)), dma((nd,)),
-            dma((3, nu)), dma((3, nu)), dma((LAYERS - 1, most, nu)), dma((LAYERS - 1, most, nu)),
+            dma((3, nu)), dma((3, nu)), dma((LAYERS - 1, most, nu)), dma((LAYERS - 1, most, nu)), dma((most, nu)),
         ],
         compiler_params=pltpu.CompilerParams(
             collective_id=0, has_side_effects=True, vmem_limit_bytes=60 * 1024 * 1024
@@ -378,7 +398,7 @@
     fits = (
         frames == 1
         and nb > 1
-        and nu > 1
+        and nu % 2 == 0
         and heads % (nb * nu) == 0
         and (rows * cols) % 8 == 0
         and size % 128 == 0

time: 39.6 us -> 39.9 us (level)
  Pallas kernels: 38.1 us -> 39.2 us
  local copies, waits for them, and re-layouts: 1.38 us -> 0.62 us
    pallas_call x1, Pallas kernels: 38.1 us -> 39.2 us  [body_fused(): pl.pallas_call(functools.partial(fused_kernel, (nb, nu, hp, size, own, wi...]
    unnamed x1, local copies, waits for them, and re-layouts: 1.38 us -> 0.62 us
where the time goes in v3:
time: 39.9 us; the launch traced here: 39.8 us
  Pallas kernels  39.2 us (98%)
  local copies, waits for them, and re-layouts  0.62 us (2%)
    pallas_call x1, Pallas kernels, body_fused(): pl.pallas_call(functools.partial(fused_kernel, (nb, nu, hp, size, own, wi...  39.2 us

profile of v3, /device:TPU:0, one launch (start us, length us, event | category | flops | bytes accessed | tf_op | source)
XLA Modules:
  0.0 39.8 jit_solution(14729022066395627987)
XLA Ops:
  0.0 39.2 %shard_map.64 = bf16[128,128]{1,0:T(8,128)(2,1)S(1)} custom-call(bf16[768,128]{1,0:T(8,128)(2,1)} %bitcast.7, bf16[16,256,256]{2,1,0:T(8,128)(2,1)} %bitcast.6, bf16[64,128]{1,0:T(8,128)(2,1)} %lift_w.1, bf16[4,3,384,512]{3,2,1,0:T(8,128)(2,1)} %bitcast.5, bf16[384,96]{1,0:T(8,128)(2,1)} %constant.4.clone.sel, bf16[384,256]{1,0:T(8,128)(2,1)} %constant.5.clone.keep), custom_call_target="tpu_custom_call" | custom-call | tf_op jit(solution)/shard_map/pallas_call | solution.py:353
  39.2 0.6 %copy.8 = bf16[1,4,32,128]{3,2,1,0:T(8,128)(2,1)} copy(bf16[1,4,32,128]{3,2,1,0:T(8,128)(2,1)S(1)} %bitcast.4) | data formatting | bytes 65536

commit v4 on v2

--- a/solution.py
+++ b/solution.py
@@ -113,6 +113,7 @@
     return current
 
 
+SPLIT = ()
 MESH = pl.DeviceIdType.MESH
 NT = (((1,), (1,)), ((), ()))
 
@@ -121,6 +122,11 @@
     return pltpu.make_async_remote_copy(
         src_ref=src, dst_ref=dst, send_sem=send, recv_sem=recv, device_id=target, device_id_type=MESH
     )
+
+
+def plan(layer, rows):
+    half = rows // 2 if layer in SPLIT else rows
+    return [0, half] + ([rows] if half < rows else [])
 
 
 def fused_kernel(
@@ -128,7 +134,7 @@
     qkv_raw, qkv_wide, qkv_mine, qkv_all, out_v, lift_all, conv_v, sel_v, keep_v, att_mine, att_all, patch_mine, patch_all, x0, acts,
     local_sem, q_send, q_recv, l_send, l_recv, a_send, a_recv, p_send, p_recv, c_send, c_recv,
 ):
-    nb, nu, hp, size, own, width, step = cfg
+    nb, nu, hp, size, own, width = cfg
     nd = nb * nu
     blk, uly = lax.axis_index("blk"), lax.axis_index("uly")
     me = blk * nu + uly
@@ -250,15 +256,15 @@
 
     for layer in range(LAYERS):
         edge = LAYERS - 1 - layer
-        span = step * width
         conv_loads[layer].wait()
-        chunks = (own + 2 * edge) // step
+        cuts = plan(layer, own + 2 * edge)
+        before = plan(layer - 1, own + 2 * edge + 2)
         ready = 0
-        for chunk in range(chunks):
-            base = chunk * span
+        for chunk in range(len(cuts) - 1):
+            base, span = cuts[chunk] * width, (cuts[chunk + 1] - cuts[chunk]) * width
             if layer > 0:
-                while ready * step < (chunk + 1) * step + 2:
-                    rows = slice(ready * span, (ready + 1) * span)
+                while before[ready] < cuts[chunk + 1] + 2:
+                    rows = slice(before[ready] * width, before[ready + 1] * width)
                     for peer in peers:
                         part = acts[layer - 1].at[peer, rows]
                         remote(
@@ -320,8 +326,7 @@
     nd, count = nb * nu, rows * cols
     hp = heads // nd
     own, width = PATCH * rows, PATCH * cols * nu
-    step = 2
-    most = (own + 2 * LAYERS) // step
+    most = 2
     latent_ch, outs = lift_weight.shape
     channels = conv_weight.shape[4]
     feats = out_weight.shape[1]
@@ -331,8 +336,8 @@
     dma = pltpu.SemaphoreType.DMA
     anywhere = pl.BlockSpec(memory_space=pl.ANY)
     pixels = pl.pallas_call(
-        functools.partial(fused_kernel, (nb, nu, hp, size, own, width, step)),
-        out_shape=jax.ShapeDtypeStruct((own * width, outs), bf16),
+        functools.partial(fused_kernel, (nb, nu, hp, size, own, width)),
+        out_shape=pltpu.VMEM((own * width, outs), bf16),
         in_specs=[anywhere] * 6,
         out_specs=pl.BlockSpec(memory_space=pltpu.VMEM),
         scratch_shapes=[
@@ -384,7 +389,6 @@
         and size % 128 == 0
         and lift_weight.shape[1] % 128 == 0
         and PATCH * rows >= LAYERS
-        and PATCH * rows % 2 == 0
         and width % 16 == 0
         and width & (width - 1) == 0
     )

time: 39.6 us -> 38.9 us (0.982)
  local copies, waits for them, and re-layouts: 1.38 us -> 0.62 us
    unnamed x1, local copies, waits for them, and re-layouts: 1.38 us -> 0.62 us
where the time goes in v4:
time: 38.9 us; the launch traced here: 38.6 us
  Pallas kernels  38 us (98%)
  local copies, waits for them, and re-layouts  0.62 us (2%)
    pallas_call x1, Pallas kernels, body_fused(): pl.pallas_call(functools.partial(fused_kernel, (nb, nu, hp, size, own, wi...  38 us

profile of v4, /device:TPU:0, one launch (start us, length us, event | category | flops | bytes accessed | tf_op | source)
XLA Modules:
  0.0 38.6 jit_solution(3494740919760023419)
XLA Ops:
  0.0 38.0 %shard_map.64 = bf16[128,128]{1,0:T(8,128)(2,1)S(1)} custom-call(bf16[768,128]{1,0:T(8,128)(2,1)} %bitcast.7, bf16[16,256,256]{2,1,0:T(8,128)(2,1)} %bitcast.6, bf16[64,128]{1,0:T(8,128)(2,1)} %lift_w.1, bf16[4,3,384,512]{3,2,1,0:T(8,128)(2,1)} %bitcast.5, bf16[384,96]{1,0:T(8,128)(2,1)} %constant.4.clone.sel, bf16[384,256]{1,0:T(8,128)(2,1)} %constant.5.clone.keep), custom_call_target="tpu_custom_call" | custom-call | tf_op jit(solution)/shard_map/pallas_call | solution.py:338
  38.0 0.6 %copy.8 = bf16[1,4,32,128]{3,2,1,0:T(8,128)(2,1)} copy(bf16[1,4,32,128]{3,2,1,0:T(8,128)(2,1)S(1)} %bitcast.4) | data formatting | bytes 65536
